TPU v7x, 128 devices: a whole 4x4x4 slice. The times are simulated.
128 devices in a mesh: dp: 32 (over z, x, core), rep: 4 (over y).
Axes of the slice: x: 4, y: 4, z: 4, core: 2. Of those that a mesh axis runs over, the one named last changes fastest.
Arguments:
- token_inputs: bfloat16 [65536, 2048], P(('dp', 'rep')), may hold values from -12 to 12
- cotangent: bfloat16 [65536, 2048], P(('dp', 'rep')), may hold values from -24 to 24
- gate_preact: bfloat16 [65536, 768], P(('dp', 'rep')), may hold values from -6 to 6
- up_preact: bfloat16 [65536, 768], P(('dp', 'rep')), may hold values from -6 to 6
- down_weight: bfloat16 [2, 768, 2048], P(None, None, 'dp'), may hold values from -0.21875 to 0.21875
- block_expert: int32 [512], P(('dp', 'rep')), may hold values from 0 to 1
- block_count: int32 [512], P(('dp', 'rep')), may hold values from 1 to 128, as said below
Outputs:
- update: bfloat16 [2, 3, 768, 2048], P(None, None, None, 'dp')
Inputs may be any that keep to these rules, and one draw needn't show every extreme that they name: `block_count`: live rows of a block, at most 128; in every draw some block is full.
All inputs are finite; a program needn't handle non-finite values.
Results may differ from a plain program's by a relative error of at most 0.02.
Values may be sent and summed in bfloat16 or wider, within the bound.
No kernel may reach another device: no remote copies, remote signals or barrier semaphores. Data moves between devices by JAX's collectives and lax.ppermute only.
A program may use at most 128 MiB of HBM per device.

v0:
```python
import math
import jax
import jax.numpy as jnp
from jax import lax
from jax.sharding import Mesh
from jax.sharding import PartitionSpec as P

D = 2048
ITERS = 2
DP = ("dp_0", "dp_1", "dp_2")
DP_REP = ("dp_0", "dp_1", "dp_2", "rep")
ns_first = 3.4445
ns_second = -4.775
ns_third = 2.0315
norm_eps = 1e-07


def cut_along(value, dim, count):
    shape = value.shape
    blocks = value.reshape(*shape[:dim], count, shape[dim] // count, *shape[dim + 1 :])
    return jnp.moveaxis(blocks, dim, 0)


def sum_by_chip(value, chips, core, dim):
    sizes = (lax.axis_size(chips), lax.axis_size(core))
    blocks = cut_along(value, dim, sizes[0] * sizes[1])
    inside = blocks.shape[1:]
    blocks = blocks.reshape(*sizes, *inside).swapaxes(0, 1).reshape(-1, *inside)
    blocks = lax.psum_scatter(blocks, core, scatter_dimension=0, tiled=True)
    return lax.psum_scatter(blocks, chips, scatter_dimension=0, tiled=True)[0]


def copy_for_each(value, axis):
    count = lax.axis_size(axis)
    return lax.all_to_all(
        jnp.broadcast_to(value[None], (count, *value.shape)), axis, 0, 0, tiled=True
    )


def of_everyone(value, axis):
    everything = copy_for_each(value, axis)
    return jnp.sum(everything.astype(jnp.float32), axis=0)


def taken_together(value, axis):
    everything = copy_for_each(value, axis)
    return jnp.sum(everything, axis=0)


def whole_sweeps(matrix, column_width, groups_all, sweeps, scale):
    hidden_width = matrix.shape[0]
    group = math.gcd(8, groups_all)
    current = matrix
    result = None
    for sweep in range(sweeps):

        def add_group(index, total):
            cols = lax.dynamic_slice_in_dim(
                current, index * group * column_width, group * column_width, 1
            )
            cols = cols.reshape(hidden_width, group, column_width)
            term = jnp.einsum(
                "fnd,gnd->nfg", cols, cols, preferred_element_type=jnp.float32
            ).astype(jnp.bfloat16)
            return total + jnp.sum(lax.optimization_barrier(term).astype(jnp.float32), axis=0)

        gram = lax.fori_loop(
            0, groups_all // group, add_group, jnp.zeros((hidden_width, hidden_width), jnp.float32)
        )
        gram_half = gram.astype(jnp.bfloat16)
        squared = jnp.dot(gram_half, gram_half, preferred_element_type=jnp.float32)
        poly = (ns_second * gram + ns_third * squared).astype(jnp.bfloat16)
        newer = ns_first * current.astype(jnp.float32) + jnp.dot(
            poly, current, preferred_element_type=jnp.float32
        )
        if sweep + 1 < sweeps:
            current = newer.astype(jnp.bfloat16)
        else:
            result = (scale * newer).astype(jnp.bfloat16)
    return result


def per_device(
    token_inputs, cotangent, gate_preact, up_preact, down_weight, block_expert, block_count
):
    blocks = block_count.shape[0]
    rows_here = token_inputs.shape[0]
    hidden_width = gate_preact.shape[1]
    width = token_inputs.shape[1]
    block_rows = rows_here // blocks
    experts_here = down_weight.shape[0]
    row_place = jnp.arange(rows_here, dtype=jnp.int32) % block_rows
    row_count = jnp.repeat(block_count, block_rows, total_repeat_length=rows_here)
    row_expert = jnp.repeat(block_expert, block_rows, total_repeat_length=rows_here)
    live_rows = row_place < row_count
    masked = jnp.where(live_rows[:, None], cotangent, jnp.zeros_like(cotangent))
    gate = gate_preact.astype(jnp.float32)
    upper = up_preact.astype(jnp.float32)
    sigmoid_gate = jax.nn.sigmoid(gate)
    hidden = (gate * sigmoid_gate * upper).astype(jnp.bfloat16)
    selector = (row_expert[None, :] == jnp.arange(experts_here, dtype=jnp.int32)[:, None]).astype(
        jnp.bfloat16
    )
    masked_each = masked[None, :, :] * selector[:, :, None]
    weights_all = lax.all_gather(down_weight, DP, axis=2, tiled=True)
    back = jnp.einsum("erd,efd->rf", masked_each, weights_all, preferred_element_type=jnp.float32)
    grad_gate = (back * upper * sigmoid_gate * (1.0 + gate * (1.0 - sigmoid_gate))).astype(
        jnp.bfloat16
    )
    grad_up = (back * gate * sigmoid_gate).astype(jnp.bfloat16)
    gate_up = jnp.concatenate([grad_gate, grad_up], axis=1)
    gate_up_each = gate_up[None, :, :] * selector[:, :, None]
    hidden_each = hidden[None, :, :] * selector[:, :, None]
    input_part = jnp.einsum(
        "erf,rd->efd", gate_up_each, token_inputs, preferred_element_type=jnp.float32
    )
    output_part = jnp.einsum("erf,rd->efd", hidden_each, masked, preferred_element_type=jnp.float32)
    partial_value = jnp.concatenate(
        [input_part.reshape(experts_here, 2, hidden_width, width), output_part[:, None]], axis=1
    )
    partial_half = partial_value.astype(jnp.bfloat16)
    terms = lax.optimization_barrier(partial_half).astype(jnp.float32)
    grad = sum_by_chip(terms.astype(jnp.bfloat16), ("dp_0", "dp_1"), "dp_2", 3).astype(jnp.float32)
    grad = of_everyone(grad.astype(jnp.bfloat16), "rep").astype(jnp.float32)
    squares = taken_together(jnp.sum(grad * grad, axis=(2, 3)), DP)
    current = (grad / (jnp.sqrt(squares) + norm_eps)[:, :, None, None]).astype(jnp.bfloat16)
    column_width = current.shape[3]
    scale = jnp.sqrt(jnp.float32(D))
    result = None
    n_dp = lax.axis_size(DP)
    matrices = experts_here * 3
    flat = current.reshape(matrices, hidden_width, column_width)
    padding = jnp.zeros((n_dp - matrices, hidden_width, column_width), jnp.bfloat16)
    outbound = jnp.concatenate([flat, padding], axis=0)
    owned = lax.all_to_all(outbound, DP, split_axis=0, concat_axis=2, tiled=True)
    finished = whole_sweeps(owned[0], column_width, n_dp, ITERS, scale)
    returned = lax.all_to_all(finished[None], DP, split_axis=2, concat_axis=0, tiled=True)
    result = returned[:matrices].reshape(experts_here, 3, hidden_width, column_width)
    return result


def solution(mesh):
    torus = Mesh(mesh.devices.reshape(4, 4, 2, mesh.shape["rep"]), ("dp_0", "dp_1", "dp_2", "rep"))
    return jax.shard_map(
        per_device,
        mesh=torus,
        in_specs=(
            P(DP_REP, None),
            P(DP_REP, None),
            P(DP_REP, None),
            P(DP_REP, None),
            P(None, None, DP),
            P(DP_REP),
            P(DP_REP),
        ),
        out_specs=P(None, None, None, DP),
        check_vma=False,
    )
```

profile of v0, /device:TPU:1, one launch (start us, length us, event | category | flops | bytes accessed | tf_op | source)
XLA Modules:
  0.0 566.8 jit_solution(1773095210929279019)
XLA Ops:
  15.2 3.2 broadcast_select_fusion
  18.3 44.0 %all-gather.2.cloned.1.call-done = bf16[2,768,2048]{1,2,0:T(8,128)(2,1)} async-done(((bf16[2,768,64]{1,2,0:T(8,128)(2,1)}), bf16[2,768,2048]{1,2,0:T(8,128)(2,1)}) %all-gather.2.cloned.1.call-update) | async-done | bytes 6291472 | tf_op jit(solution)/shard_map/all_gather | solution.py:105
  62.4 7.8 %fusion.10 = (bf16[512,768]{1,0:T(8,128)(2,1)S(1)}, bf16[512,768]{1,0:T(8,128)(2,1)S(1)}, bf16[512,768]{1,0:T(8,128)(2,1)S(1)}) fusion(bf16[512,768]{1,0:T(8,128)(2,1)} %param.20, bf16[512,768]{1,0:T(8,128)(2,1)} %param.19, bf16[2,768,2048]{1,2,0:T(8,128)(2,1)} %all-gather.2.cloned.1.call-done, bf16[2,512]{1,0:T(2,128)(2,1)S(1)} %compare_convert_fusion, ...), kind=kOutput, calls=%fused_computation.33 | convolution fusion | flops 3230400512 | bytes 12322816 | tf_op jit(solution)/shard_map/erd,efd->rf/dot_general | solution.py:106
  74.0 10.6 %convolution_convert_fusion.2 = bf16[2,1536,2048]{2,1,0:T(8,128)(2,1)} fusion(bf16[512,2048]{1,0:T(8,128)(2,1)S(1)} %copy-done, bf16[2,512]{1,0:T(2,128)(2,1)S(1)} %compare_convert_fusion, bf16[512,1536]{0,1:T(8,128)(2,1)} %copy.51), kind=kOutput, calls=%fused_computation.9 | convolution fusion | flops 6450315264 | bytes 16254976 | tf_op jit(solution)/shard_map/erf,rd->efd/dot_general | solution.py:114
  84.7 16.8 %copy.53 = bf16[2,2,768,2048]{2,3,1,0:T(8,128)(2,1)} copy(bf16[2,2,768,2048]{3,2,1,0:T(8,128)(2,1)} %bitcast.100) | data formatting | bytes 25165824 | tf_op jit(solution)/shard_map/reshape | solution.py:119
  102.6 6.3 %convert_bitcast_fusion = bf16[2,1,768,2048]{3,2,0,1:T(8,128)(2,1)} fusion(bf16[512,2048]{1,0:T(8,128)(2,1)S(1)} %copy-done.2, bf16[2,512]{1,0:T(2,128)(2,1)S(1)} %compare_convert_fusion, bf16[512,768]{0,1:T(8,128)(2,1)} %copy.52), kind=kOutput, calls=%fused_computation.12 | convolution fusion | flops 3225157632 | bytes 9177088 | tf_op jit(solution)/shard_map/erf,rd->efd/dot_general | solution.py:117
  108.9 8.7 %copy.54 = bf16[2,1,768,2048]{2,3,1,0:T(8,128)(2,1)} copy(bf16[2,1,768,2048]{3,2,0,1:T(8,128)(2,1)} %convert_bitcast_fusion) | data formatting | bytes 12582912 | tf_op jit(solution)/shard_map/broadcast_in_dim | solution.py:119
  117.6 9.5 %pad_maximum_fusion = bf16[2,3,768,2048]{2,3,1,0:T(8,128)(2,1)S(1)} fusion(bf16[2,1,768,2048]{2,3,1,0:T(8,128)(2,1)} %copy.54, bf16[2,2,768,2048]{2,3,1,0:T(8,128)(2,1)} %copy.53), kind=kLoop, calls=%fused_computation.8 | loop fusion | flops 9437184 | bytes 37748736 | tf_op jit(solution)/shard_map/concatenate | solution.py:118
  127.1 6.7 %copy.55 = bf16[16,2,2,3,768,64]{4,5,3,2,0,1:T(8,128)(2,1)} copy(bf16[16,2,2,3,768,64]{4,5,1,0,3,2:T(8,128)(2,1)S(1)} %bitcast.97) | data formatting | bytes 37748736 | tf_op jit(solution)/shard_map/reshape | solution.py:28
  133.9 28.0 %reduce-scatter.5.cloned.1.call-done = bf16[16,2,3,768,64]{3,4,2,1,0:T(8,128)(2,1)} async-done(((bf16[32,2,3,768,64]{3,4,2,1,0:T(8,128)(2,1)}), bf16[16,2,3,768,64]{3,4,2,1,0:T(8,128)(2,1)}) %reduce-scatter.5.cloned.1.call-update) | async-done | bytes 9437200 | tf_op jit(solution)/shard_map/reduce_scatter | solution.py:29
  161.9 91.3 %reduce-scatter.7.cloned.1.call-done = bf16[1,2,3,768,64]{3,4,2,1,0:T(8,128)(2,1)} async-done(((bf16[16,2,3,768,64]{3,4,2,1,0:T(8,128)(2,1)}), bf16[1,2,3,768,64]{3,4,2,1,0:T(8,128)(2,1)}) %reduce-scatter.7.cloned.1.call-update) | async-done | bytes 589840
  254.5 30.7 %all_to_all.40 = bf16[4,2,3,768,64]{3,4,2,1,0:T(8,128)(2,1)S(1)} all-to-all(bf16[4,2,3,768,64]{3,4,2,1,0:T(8,128)(2,1)S(1)} %broadcast_in_dim.31), channel_id=1, replica_groups=mesh['dp_0'=4,'dp_1'=4,'dp_2'=2,'rep'=4] {'rep'}, dimensions={0} | all-to-all | bytes 4718592 | tf_op jit(solution)/shard_map/all_to_all | solution.py:35
  285.8 15.0 %all_to_all.41 = f32[32,2,3]{2,1,0:T(2,128)S(1)} all-to-all(f32[32,2,3]{2,1,0:T(2,128)S(1)} %broadcast_in_dim.32), channel_id=1, replica_groups=mesh['dp_0'=4,'dp_1'=4,'dp_2'=2,'rep'=4] {'dp_0','dp_1','dp_2'}, dimensions={0} | all-to-all | bytes 1536 | tf_op jit(solution)/shard_map/all_to_all | solution.py:35
  303.3 5.0 all-to-all-start.2
  308.3 39.9 %all-to-all-done.2 = bf16[32,768,64]{1,2,0:T(8,128)(2,1)} async-done(((bf16[32,768,64]{1,2,0:T(8,128)(2,1)}), bf16[32,768,64]{1,2,0:T(8,128)(2,1)}, u32[]{:S(2)}, u32[]{:S(2)}) %all-to-all-start.2) | async-done | bytes 3145760 | tf_op jit(solution)/shard_map/all_to_all | solution.py:135
  348.2 4.7 copy.58
  352.9 33.6 %while.34 = (s32[]{:T(128)}, f32[768,768]{1,0:T(8,128)}, bf16[768,2048]{0,1:T(8,128)(2,1)}, s32[]{:T(128)}, s32[]{:T(128)}, /*index=5*/s32[]{:T(128)}, s32[]{:T(128)}) while((s32[]{:T(128)}, f32[768,768]{1,0:T(8,128)}, bf16[768,2048]{0,1:T(8,128)(2,1)}, s32[]{:T(128)}, s32[]{:T(128)}, /*index=5*/s32[]{:T(128)}, s32[]{:T(128)}) %tuple.98), condition=%wide.region_7.9_spmd.clone, body=%wide.region_5.8_spmd.clone.sunk | while | flops 618725376 | bytes 30670984 | solution.py:67
  365.4 3.4 select_add_fusion.4
  374.2 3.4 select_add_fusion.4
  383.0 3.4 select_add_fusion.4
  386.5 10.5 %add_convert_fusion = bf16[768,2048]{1,0:T(8,128)(2,1)} fusion(bf16[768,2048]{1,0:T(8,128)(2,1)} %copy.58, bf16[768,2048]{0,1:T(8,128)(2,1)} %bitcast.23, f32[768,768]{1,0:T(8,128)} %get-tuple-element.202), kind=kOutput, calls=%fused_computation.11 | convolution fusion | flops 3331129344 | bytes 11796480 | tf_op jit(solution)/shard_map/dot_general | solution.py:73
  397.0 34.4 %while.35 = (s32[]{:T(128)}, f32[768,768]{1,0:T(8,128)}, bf16[768,2048]{1,0:T(8,128)(2,1)}, s32[]{:T(128)}, s32[]{:T(128)}, /*index=5*/s32[]{:T(128)}, s32[]{:T(128)}) while((s32[]{:T(128)}, f32[768,768]{1,0:T(8,128)}, bf16[768,2048]{1,0:T(8,128)(2,1)}, s32[]{:T(128)}, s32[]{:T(128)}, /*index=5*/s32[]{:T(128)}, s32[]{:T(128)}) %tuple.101), condition=%wide.region_10.12_spmd.clone, body=%wide.region_8.11_spmd.clone.sunk | while | flops 618725376 | bytes 32243848 | solution.py:67
  410.0 3.4 select_add_fusion.5
  419.0 3.4 select_add_fusion.5
  428.0 3.4 select_add_fusion.5
  431.4 8.5 %fusion.3 = bf16[1,768,2048]{2,1,0:T(8,128)(2,1)S(1)} fusion(bf16[768,2048]{1,0:T(8,128)(2,1)} %get-tuple-element.360, f32[768,768]{1,0:T(8,128)} %get-tuple-element.203), kind=kOutput, calls=%fused_computation.17 | convolution fusion | flops 3332702208 | bytes 8650752 | tf_op jit(solution)/shard_map/dot_general | solution.py:73
  439.9 11.2 %copy.60 = bf16[1,768,2048]{1,0,2:T(2,128)(2,1)} copy(bf16[1,768,2048]{2,1,0:T(8,128)(2,1)S(1)} %fusion.3) | data formatting | bytes 6291456 | tf_op jit(solution)/shard_map/broadcast_in_dim | solution.py:137
  451.7 33.3 %reduce.3 = bf16[2048,768]{1,0:T(8,128)(2,1)} reduce(bf16[2048,1,768]{2,1,0:T(2,128)(2,1)} %bitcast.98, bf16[]{:T(256)} %broadcast.220), dimensions={1}, to_apply=%bitcast.73.reduce_sub_computation | reduce | bytes 6291458
  485.0 6.6 %reshape.174 = bf16[32,2,24576]{2,1,0:T(2,128)(2,1)S(1)} reshape(bf16[2048,768]{1,0:T(8,128)(2,1)} %reduce.3) | data formatting | bytes 6291456
  491.6 45.5 %all_to_all.42 = bf16[32,2,24576]{2,1,0:T(2,128)(2,1)} all-to-all(bf16[32,2,24576]{2,1,0:T(2,128)(2,1)S(1)} %reshape.174), channel_id=1, replica_groups=mesh['dp_0'=4,'dp_1'=4,'dp_2'=2,'rep'=4] {'dp_0','dp_1','dp_2'}, dimensions={0} | all-to-all | bytes 6291456 | tf_op jit(solution)/shard_map/all_to_all | solution.py:137
  537.1 18.9 %reshape.175 = bf16[2048,1,768]{2,1,0:T(2,128)(2,1)} reshape(bf16[32,2,24576]{2,1,0:T(2,128)(2,1)} %all_to_all.42) | data formatting | bytes 6291456
  556.0 3.5 copy.62
  (65 shorter events, 66.9 us)
Async XLA Ops:
  6.5 67.5 %copy-start = (bf16[512,2048]{1,0:T(8,128)(2,1)S(1)}, bf16[512,2048]{1,0:T(8,128)(2,1)}, u32[]{:S(2)}) copy-start(bf16[512,2048]{1,0:T(8,128)(2,1)} %param.17) | copy-start | bytes 6291460
  6.5 55.8 %all-gather.2.cloned.1.call-start = ((), (), s32[]{:S(2)}) async-start(), calls=%async_computation.6 | async-start | bytes 6488064 | tf_op jit(solution)/shard_map/all_gather | solution.py:105
  7.3 154.6 %reduce-scatter.5.cloned.1.call-start = ((), (), s32[]{:S(2)}) async-start(), calls=%async_computation.7 | async-start | bytes 28311552 | tf_op jit(solution)/shard_map/reduce_scatter | solution.py:29
  84.7 18.0 %copy-start.2 = (bf16[512,2048]{1,0:T(8,128)(2,1)S(1)}, bf16[512,2048]{1,0:T(8,128)(2,1)}, u32[]{:S(2)}) copy-start(bf16[512,2048]{1,0:T(8,128)(2,1)} %broadcast_select_fusion) | copy-start | bytes 6291460
  133.8 119.4 %reduce-scatter.7.cloned.1.call-start = ((), (), s32[]{:S(2)}) async-start(), calls=%async_computation.8 | async-start | bytes 10027008
  303.3 44.9 %all-to-all-start.2 = ((bf16[32,768,64]{1,2,0:T(8,128)(2,1)}), bf16[32,768,64]{1,2,0:T(8,128)(2,1)}, u32[]{:S(2)}, u32[]{:S(2)}) async-start(bf16[32,768,64]{1,2,0:T(8,128)(2,1)} %concatenate.18), calls=%async_computation.3 | async-start | bytes 6291456 | tf_op jit(solution)/shard_map/all_to_all | solution.py:135
  556.0 4.3 copy-start.1
Sparse Core Ops, SparseCore 0:
  9.6 52.6 all-gather.1
  133.9 27.9 reduce-scatter.4
  165.4 87.7 reduce-scatter.6
where the time goes:
time: 570 us; the launch traced here: 567 us
  waiting for transfers between devices  204 us (36%)
  local copies, waits for them, and re-layouts  99.3 us (17%)
  blocking collectives  91.1 us (16%)
  other arithmetic  87 us (15%)
  matrix products  66.9 us (12%)
  between operations  13.2 us (2%)
    unnamed x4, waiting for transfers between devices  92 us
    all_to_all x2, blocking collectives, copy_for_each(): lax.all_to_all(jnp.broadcast_to(value[None], (count, *value.shape)), axis...  45.6 us
    all_to_all x1, blocking collectives, per_device(): lax.all_to_all(finished[None], DP, split_axis=2, concat_axis=0, tiled=True)  45.5 us
    all_gather x1, waiting for transfers between devices, per_device(): weights_all = lax.all_gather(down_weight, DP, axis=2, tiled=True)  44 us
    all_to_all x1, waiting for transfers between devices, per_device(): lax.all_to_all(outbound, DP, split_axis=0, concat_axis=2, tiled=True)  39.9 us
    unnamed x3, other arithmetic  33.3 us
    unnamed x11, local copies, waits for them, and re-layouts  29.6 us
    reduce_scatter x1, waiting for transfers between devices, sum_by_chip(): blocks = lax.psum_scatter(blocks, core, scatter_dimension=0, tiled=True)  28 us
  transfers between devices with their start and end apart: 4, of which 4 were waited for; matrix products, arithmetic and copies ran while one was open for 2% of the time, Pallas kernels for 0%

commit v1 on v0

--- a/solution.py
+++ b/solution.py
@@ -102,7 +102,9 @@
         jnp.bfloat16
     )
     masked_each = masked[None, :, :] * selector[:, :, None]
-    weights_all = lax.all_gather(down_weight, DP, axis=2, tiled=True)
+    weights_all = jnp.concatenate(
+        lax.all_to_all(jnp.stack([down_weight] * lax.axis_size(DP)), DP, 0, 0), axis=2
+    )
     back = jnp.einsum("erd,efd->rf", masked_each, weights_all, preferred_element_type=jnp.float32)
     grad_gate = (back * upper * sigmoid_gate * (1.0 + gate * (1.0 - sigmoid_gate))).astype(
         jnp.bfloat16

time: 570 us -> 605 us (1.061)
  waiting for transfers between devices: 204 us -> 226 us
  starting transfers between devices: 5.05 us -> 14.5 us
  local copies, waits for them, and re-layouts: 99.3 us -> 106 us
    all_to_all x0 -> x1, waiting for transfers between devices: none -> 63.9 us  [per_device(): lax.all_to_all(jnp.stack([down_weight] * lax.axis_size(DP)), DP, 0, 0)]
    all_gather x1 -> x0, waiting for transfers between devices: 44 us -> none  [per_device(): weights_all = lax.all_gather(down_weight, DP, axis=2, tiled=True)]
    all_to_all x0 -> x1, starting transfers between devices: none -> 9.6 us  [per_device(): lax.all_to_all(jnp.stack([down_weight] * lax.axis_size(DP)), DP, 0, 0)]
    unnamed x4 -> x3, waiting for transfers between devices: 92 us -> 91.4 us
    unnamed x11 -> x21, local copies, waits for them, and re-layouts: 29.6 us -> 30 us
where the time goes in v1:
time: 605 us; the launch traced here: 602 us
  waiting for transfers between devices  226 us (37%)
  local copies, waits for them, and re-layouts  106 us (18%)
  blocking collectives  91.5 us (15%)
  other arithmetic  87.1 us (14%)
  matrix products  63.2 us (10%)
  starting transfers between devices  14.5 us (2%)
  between operations  13.6 us (2%)
    unnamed x3, waiting for transfers between devices  91.4 us
    all_to_all x1, waiting for transfers between devices, per_device(): lax.all_to_all(jnp.stack([down_weight] * lax.axis_size(DP)), DP, 0, 0)  63.9 us
    all_to_all x1, blocking collectives, per_device(): lax.all_to_all(finished[None], DP, split_axis=2, concat_axis=0, tiled=True)  45.8 us
    all_to_all x2, blocking collectives, copy_for_each(): lax.all_to_all(jnp.broadcast_to(value[None], (count, *value.shape)), axis...  45.7 us
    all_to_all x1, waiting for transfers between devices, per_device(): lax.all_to_all(outbound, DP, split_axis=0, concat_axis=2, tiled=True)  39.5 us
    unnamed x3, other arithmetic  33.3 us
    reduce_scatter x1, waiting for transfers between devices, sum_by_chip(): blocks = lax.psum_scatter(blocks, core, scatter_dimension=0, tiled=True)  30.7 us
    unnamed x21, local copies, waits for them, and re-layouts  30 us
  transfers between devices with their start and end apart: 4, of which 4 were waited for; matrix products, arithmetic and copies ran while one was open for 2% of the time, Pallas kernels for 0%

profile of v1, /device:TPU:1, one launch (start us, length us, event | category | flops | bytes accessed | tf_op | source)
XLA Modules:
  0.0 601.8 jit_solution(14223609903028535106)
XLA Ops:
  6.5 4.5 stack.2
  11.0 9.6 %all-to-all-start = ((bf16[32,2,768,64]{2,3,1,0:T(8,128)(2,1)}), bf16[32,2,768,64]{2,3,1,0:T(8,128)(2,1)}, u32[]{:S(2)}, u32[]{:S(2)}) async-start(bf16[32,2,768,64]{2,3,1,0:T(8,128)(2,1)} %stack.2), calls=%async_computation | async-start | bytes 12582912 | tf_op jit(solution)/shard_map/all_to_all | solution.py:106
  30.4 63.9 %all-to-all-done = bf16[32,2,768,64]{2,3,1,0:T(8,128)(2,1)} async-done(((bf16[32,2,768,64]{2,3,1,0:T(8,128)(2,1)}), bf16[32,2,768,64]{2,3,1,0:T(8,128)(2,1)}, u32[]{:S(2)}, u32[]{:S(2)}) %all-to-all-start) | async-done | bytes 6291488 | tf_op jit(solution)/shard_map/all_to_all | solution.py:106
  98.1 4.1 fusion.10
  106.1 10.6 %convolution_convert_fusion.2 = bf16[2,1536,2048]{2,1,0:T(8,128)(2,1)} fusion(bf16[512,2048]{1,0:T(8,128)(2,1)S(1)} %copy-done, bf16[2,512]{1,0:T(2,128)(2,1)S(1)} %compare_convert_fusion, bf16[512,1536]{0,1:T(8,128)(2,1)} %copy.61), kind=kOutput, calls=%fused_computation.9 | convolution fusion | flops 6450315264 | bytes 16254976 | tf_op jit(solution)/shard_map/erf,rd->efd/dot_general | solution.py:116
  116.7 16.8 %copy.63 = bf16[2,2,768,2048]{2,3,1,0:T(8,128)(2,1)} copy(bf16[2,2,768,2048]{3,2,1,0:T(8,128)(2,1)} %bitcast.103) | data formatting | bytes 25165824 | tf_op jit(solution)/shard_map/reshape | solution.py:121
  134.7 6.3 %convert_bitcast_fusion = bf16[2,1,768,2048]{3,2,0,1:T(8,128)(2,1)} fusion(bf16[512,2048]{1,0:T(8,128)(2,1)S(1)} %copy-done.3, bf16[2,512]{1,0:T(2,128)(2,1)S(1)} %compare_convert_fusion, bf16[512,768]{0,1:T(8,128)(2,1)} %copy.62), kind=kOutput, calls=%fused_computation.12 | convolution fusion | flops 3225157632 | bytes 9177088 | tf_op jit(solution)/shard_map/erf,rd->efd/dot_general | solution.py:119
  140.9 8.7 %copy.64 = bf16[2,1,768,2048]{2,3,1,0:T(8,128)(2,1)} copy(bf16[2,1,768,2048]{3,2,0,1:T(8,128)(2,1)} %convert_bitcast_fusion) | data formatting | bytes 12582912 | tf_op jit(solution)/shard_map/broadcast_in_dim | solution.py:121
  149.6 9.5 %pad_maximum_fusion = bf16[2,3,768,2048]{2,3,1,0:T(8,128)(2,1)S(1)} fusion(bf16[2,1,768,2048]{2,3,1,0:T(8,128)(2,1)} %copy.64, bf16[2,2,768,2048]{2,3,1,0:T(8,128)(2,1)} %copy.63), kind=kLoop, calls=%fused_computation.8 | loop fusion | flops 9437184 | bytes 37748736 | tf_op jit(solution)/shard_map/concatenate | solution.py:120
  159.1 6.7 %copy.65 = bf16[16,2,2,3,768,64]{4,5,3,2,0,1:T(8,128)(2,1)} copy(bf16[16,2,2,3,768,64]{4,5,1,0,3,2:T(8,128)(2,1)S(1)} %bitcast.100) | data formatting | bytes 37748736 | tf_op jit(solution)/shard_map/reshape | solution.py:28
  165.9 30.7 %reduce-scatter.5.cloned.1.call-done = bf16[16,2,3,768,64]{3,4,2,1,0:T(8,128)(2,1)} async-done(((bf16[32,2,3,768,64]{3,4,2,1,0:T(8,128)(2,1)}), bf16[16,2,3,768,64]{3,4,2,1,0:T(8,128)(2,1)}) %reduce-scatter.5.cloned.1.call-update) | async-done | bytes 9437200 | tf_op jit(solution)/shard_map/reduce_scatter | solution.py:29
  196.6 91.4 %reduce-scatter.7.cloned.1.call-done = bf16[1,2,3,768,64]{3,4,2,1,0:T(8,128)(2,1)} async-done(((bf16[16,2,3,768,64]{3,4,2,1,0:T(8,128)(2,1)}), bf16[1,2,3,768,64]{3,4,2,1,0:T(8,128)(2,1)}) %reduce-scatter.7.cloned.1.call-update) | async-done | bytes 589840
  289.4 30.8 %all_to_all.45 = bf16[4,2,3,768,64]{3,4,2,1,0:T(8,128)(2,1)S(1)} all-to-all(bf16[4,2,3,768,64]{3,4,2,1,0:T(8,128)(2,1)S(1)} %broadcast_in_dim.31), channel_id=1, replica_groups=mesh['dp_0'=4,'dp_1'=4,'dp_2'=2,'rep'=4] {'rep'}, dimensions={0} | all-to-all | bytes 4718592 | tf_op jit(solution)/shard_map/all_to_all | solution.py:35
  320.8 14.9 %all_to_all.46 = f32[32,2,3]{2,1,0:T(2,128)S(1)} all-to-all(f32[32,2,3]{2,1,0:T(2,128)S(1)} %broadcast_in_dim.32), channel_id=1, replica_groups=mesh['dp_0'=4,'dp_1'=4,'dp_2'=2,'rep'=4] {'dp_0','dp_1','dp_2'}, dimensions={0} | all-to-all | bytes 1536 | tf_op jit(solution)/shard_map/all_to_all | solution.py:35
  338.2 4.8 all-to-all-start.3
  343.0 39.5 %all-to-all-done.3 = bf16[32,768,64]{1,2,0:T(8,128)(2,1)} async-done(((bf16[32,768,64]{1,2,0:T(8,128)(2,1)}), bf16[32,768,64]{1,2,0:T(8,128)(2,1)}, u32[]{:S(2)}, u32[]{:S(2)}) %all-to-all-start.3) | async-done | bytes 3145760 | tf_op jit(solution)/shard_map/all_to_all | solution.py:137
  382.5 4.7 copy.68
  387.2 33.6 %while.34 = (s32[]{:T(128)}, f32[768,768]{1,0:T(8,128)}, bf16[768,2048]{0,1:T(8,128)(2,1)}, s32[]{:T(128)}, s32[]{:T(128)}, /*index=5*/s32[]{:T(128)}, s32[]{:T(128)}) while((s32[]{:T(128)}, f32[768,768]{1,0:T(8,128)}, bf16[768,2048]{0,1:T(8,128)(2,1)}, s32[]{:T(128)}, s32[]{:T(128)}, /*index=5*/s32[]{:T(128)}, s32[]{:T(128)}) %tuple.98), condition=%wide.region_7.9_spmd.clone, body=%wide.region_5.8_spmd.clone.sunk | while | flops 618725376 | bytes 30670984 | solution.py:67
  399.7 3.4 select_add_fusion.4
  408.5 3.4 select_add_fusion.4
  417.4 3.4 select_add_fusion.4
  420.8 10.5 %add_convert_fusion = bf16[768,2048]{1,0:T(8,128)(2,1)} fusion(bf16[768,2048]{1,0:T(8,128)(2,1)} %copy.68, bf16[768,2048]{0,1:T(8,128)(2,1)} %bitcast.25, f32[768,768]{1,0:T(8,128)} %get-tuple-element.202), kind=kOutput, calls=%fused_computation.11 | convolution fusion | flops 3331129344 | bytes 11796480 | tf_op jit(solution)/shard_map/dot_general | solution.py:73
  431.3 34.4 %while.35 = (s32[]{:T(128)}, f32[768,768]{1,0:T(8,128)}, bf16[768,2048]{1,0:T(8,128)(2,1)}, s32[]{:T(128)}, s32[]{:T(128)}, /*index=5*/s32[]{:T(128)}, s32[]{:T(128)}) while((s32[]{:T(128)}, f32[768,768]{1,0:T(8,128)}, bf16[768,2048]{1,0:T(8,128)(2,1)}, s32[]{:T(128)}, s32[]{:T(128)}, /*index=5*/s32[]{:T(128)}, s32[]{:T(128)}) %tuple.101), condition=%wide.region_10.12_spmd.clone, body=%wide.region_8.11_spmd.clone.sunk | while | flops 618725376 | bytes 32243848 | solution.py:67
  444.3 3.4 select_add_fusion.5
  453.3 3.4 select_add_fusion.5
  465.7 8.5 %fusion.3 = bf16[1,768,2048]{2,1,0:T(8,128)(2,1)S(1)} fusion(bf16[768,2048]{1,0:T(8,128)(2,1)} %get-tuple-element.361, f32[768,768]{1,0:T(8,128)} %get-tuple-element.203), kind=kOutput, calls=%fused_computation.17 | convolution fusion | flops 3332702208 | bytes 8650752 | tf_op jit(solution)/shard_map/dot_general | solution.py:73
  474.3 11.2 %copy.70 = bf16[1,768,2048]{1,0,2:T(2,128)(2,1)} copy(bf16[1,768,2048]{2,1,0:T(8,128)(2,1)S(1)} %fusion.3) | data formatting | bytes 6291456 | tf_op jit(solution)/shard_map/broadcast_in_dim | solution.py:139
  486.0 33.3 %reduce.3 = bf16[2048,768]{1,0:T(8,128)(2,1)} reduce(bf16[2048,1,768]{2,1,0:T(2,128)(2,1)} %bitcast.101, bf16[]{:T(256)} %broadcast.222), dimensions={1}, to_apply=%bitcast.76.reduce_sub_computation | reduce | bytes 6291458
  519.3 6.6 %reshape.184 = bf16[32,2,24576]{2,1,0:T(2,128)(2,1)S(1)} reshape(bf16[2048,768]{1,0:T(8,128)(2,1)} %reduce.3) | data formatting | bytes 6291456
  525.9 45.8 %all_to_all.47 = bf16[32,2,24576]{2,1,0:T(2,128)(2,1)} all-to-all(bf16[32,2,24576]{2,1,0:T(2,128)(2,1)S(1)} %reshape.184), channel_id=1, replica_groups=mesh['dp_0'=4,'dp_1'=4,'dp_2'=2,'rep'=4] {'dp_0','dp_1','dp_2'}, dimensions={0} | all-to-all | bytes 6291456 | tf_op jit(solution)/shard_map/all_to_all | solution.py:139
  571.8 18.9 %reshape.185 = bf16[2048,1,768]{2,1,0:T(2,128)(2,1)} reshape(bf16[32,2,24576]{2,1,0:T(2,128)(2,1)} %all_to_all.47) | data formatting | bytes 6291456
  590.7 3.5 copy.73
  (76 shorter events, 75.1 us)
Async XLA Ops:
  6.5 99.5 %copy-start = (bf16[512,2048]{1,0:T(8,128)(2,1)S(1)}, bf16[512,2048]{1,0:T(8,128)(2,1)}, u32[]{:S(2)}) copy-start(bf16[512,2048]{1,0:T(8,128)(2,1)} %param.17) | copy-start | bytes 6291460
  11.0 9.7 %copy-start.4 = (s32[4]{0:T(128)S(1)}, s32[4]{0:T(128)}, u32[]{:S(2)}) copy-start(s32[4]{0:T(128)} %param.23) | copy-start | bytes 52
  11.0 12.9 %copy-start.5 = (s32[4]{0:T(128)S(1)}, s32[4]{0:T(128)}, u32[]{:S(2)}) copy-start(s32[4]{0:T(128)} %param.22) | copy-start | bytes 52
  11.0 83.2 %all-to-all-start = ((bf16[32,2,768,64]{2,3,1,0:T(8,128)(2,1)}), bf16[32,2,768,64]{2,3,1,0:T(8,128)(2,1)}, u32[]{:S(2)}, u32[]{:S(2)}) async-start(bf16[32,2,768,64]{2,3,1,0:T(8,128)(2,1)} %stack.2), calls=%async_computation | async-start | bytes 12582912 | tf_op jit(solution)/shard_map/all_to_all | solution.py:106
  20.6 176.0 %reduce-scatter.5.cloned.1.call-start = ((), (), s32[]{:S(2)}) async-start(), calls=%async_computation.7 | async-start | bytes 28311552 | tf_op jit(solution)/shard_map/reduce_scatter | solution.py:29
  94.3 3.4 copy-start.2
  94.3 3.6 copy-start.6
  94.3 3.8 copy-start.7
  116.7 18.0 %copy-start.3 = (bf16[512,2048]{1,0:T(8,128)(2,1)S(1)}, bf16[512,2048]{1,0:T(8,128)(2,1)}, u32[]{:S(2)}) copy-start(bf16[512,2048]{1,0:T(8,128)(2,1)} %broadcast_select_fusion) | copy-start | bytes 6291460
  165.8 122.2 %reduce-scatter.7.cloned.1.call-start = ((), (), s32[]{:S(2)}) async-start(), calls=%async_computation.8 | async-start | bytes 10027008
  338.2 44.3 %all-to-all-start.3 = ((bf16[32,768,64]{1,2,0:T(8,128)(2,1)}), bf16[32,768,64]{1,2,0:T(8,128)(2,1)}, u32[]{:S(2)}, u32[]{:S(2)}) async-start(bf16[32,768,64]{1,2,0:T(8,128)(2,1)} %concatenate.18), calls=%async_computation.4 | async-start | bytes 6291456 | tf_op jit(solution)/shard_map/all_to_all | solution.py:137
  590.7 4.3 copy-start.1
Sparse Core Ops, SparseCore 0:
  166.0 30.6 reduce-scatter.4
  200.1 87.8 reduce-scatter.6
